TPU v7x, 128 devices: a whole 4x4x4 slice. The times are simulated.
128 devices in a mesh: lat: 8 (over x, core), lon: 4 (over y), lev: 4 (over z).
Axes of the slice: x: 4, y: 4, z: 4, core: 2. Of those that a mesh axis runs over, the one named last changes fastest.
Arguments:
- initial_state: float32 [32, 384, 128, 128], P('lat', 'lon', 'lev'), may hold values from 0.5 to 2
- scaled_wind_north: float32 [32, 384, 128, 128], P('lat', 'lon', 'lev'), may hold values from -0.3 to 0.3
- scaled_wind_east: float32 [32, 384, 128, 128], P('lat', 'lon', 'lev'), may hold values from -0.3 to 0.3
- scaled_wind_upward: float32 [32, 384, 128, 128], P('lat', 'lon', 'lev'), may hold values from -0.3 to 0.3
Outputs:
- normalised_state: float32 [32, 384, 128, 128], P('lat', 'lon', 'lev')
- temperature_end: float32 [32, 384, 128, 128], P('lat', 'lon', 'lev')
All inputs are finite; a program needn't handle non-finite values.
Results may differ from a plain program's by a relative error of at most 0.00002.
Values sent between devices are 32-bit elements; how exact they have to be, the bound alone decides.
A program may use at most 128 MiB of HBM per device.

v0:
```python
import jax
import jax.numpy as jnp
from jax import lax
from jax.sharding import PartitionSpec as P

STEPS = 4


def padded(array, sides, width):
    edges = {}
    for axis, dim in sides:
        count, length = (lax.axis_size(axis), array.shape[dim])
        up = [(i, (i + 1) % count) for i in range(count - 1)]
        last = lax.slice_in_dim(array, length - width, length, axis=dim)
        initial = lax.slice_in_dim(array, 0, width, axis=dim)
        edges[dim] = (
            lax.ppermute(last, axis, up),
            lax.ppermute(initial, axis, [(b, a) for a, b in up]),
        )
    done = []
    for _, dim in sides:
        low, high = edges[dim]
        around = [(width, width) if d in done else (0, 0) for d in range(array.ndim)]
        array = jnp.concatenate([jnp.pad(low, around), array, jnp.pad(high, around)], axis=dim)
        done.append(dim)
    return array


def copy_for_each(array, axis):
    copies = jnp.broadcast_to(array, (lax.axis_size(axis), *array.shape))
    return lax.all_to_all(copies, axis, split_axis=0, concat_axis=0, tiled=True)


def over_copies(array, axis):
    return copy_for_each(array, axis).sum(axis=0)


def together(arrays, axis):
    ends = [0]
    for a in arrays:
        ends.append(ends[-1] + a.size)
    subtotal = over_copies(jnp.concatenate([a.ravel() for a in arrays]), axis)
    return tuple((subtotal[b:e].reshape(a.shape) for a, b, e in zip(arrays, ends, ends[1:])))


def strip_edges(values, dims):
    for dim in dims:
        values = lax.slice_in_dim(values, 1, values.shape[dim] - 1, axis=dim)
    return values


def neighbour(values, dim, start, dims):
    others = [other for other in dims if other != dim]
    values = strip_edges(values, others)
    return lax.slice_in_dim(values, start, start + values.shape[dim] - 2, axis=dim)


def march_one_step(padded_state, scaled_wind_north, scaled_wind_east, scaled_wind_upward):
    middle = strip_edges(padded_state, (0, 1, 2))
    lower = [neighbour(padded_state, dim, 0, (0, 1, 2)) for dim in (0, 1, 2)]
    upper = [neighbour(padded_state, dim, 2, (0, 1, 2)) for dim in (0, 1, 2)]
    slopes = [above - below for above, below in zip(upper, lower)]
    smooth_rate = 0.05
    spread = lower[0] + upper[0] + lower[1] + upper[1] + lower[2] + upper[2] - 6.0 * middle
    return (
        middle
        - scaled_wind_north * slopes[0]
        - scaled_wind_east * slopes[1]
        - scaled_wind_upward * slopes[2]
        + smooth_rate * spread
    )


def shards(initial_state, scaled_wind_north, scaled_wind_east, scaled_wind_upward):
    for step in range(STEPS):
        padded_state = padded(initial_state, (("lat", 0), ("lon", 1), ("lev", 2)), 1)
        initial_state = march_one_step(
            padded_state, scaled_wind_north, scaled_wind_east, scaled_wind_upward
        )
    number_of_values = initial_state.shape[1] * lax.axis_size("lon")
    guess = 1.0
    moved = initial_state - guess
    totals, squares = together(
        (jnp.sum(moved, axis=1, keepdims=True), jnp.sum(moved * moved, axis=1, keepdims=True)),
        "lon",
    )
    vertical_mean = guess + totals / number_of_values
    symmetric_slope = initial_state - vertical_mean
    line_variance = squares / number_of_values - totals / number_of_values * (
        totals / number_of_values
    )
    normalised_state = symmetric_slope * lax.rsqrt(line_variance + 0.0001)
    return (normalised_state, initial_state)


def solution(mesh):
    return jax.shard_map(
        shards,
        mesh=mesh,
        in_specs=(
            P("lat", "lon", "lev", None),
            P("lat", "lon", "lev", None),
            P("lat", "lon", "lev", None),
            P("lat", "lon", "lev", None),
        ),
        out_specs=(P("lat", "lon", "lev", None), P("lat", "lon", "lev", None)),
        check_vma=False,
    )
```

profile of v0, /device:TPU:14, one launch (start us, length us, event | category | flops | bytes accessed | tf_op | source)
XLA Modules:
  0.0 268.8 jit_solution(3711400979713692046)
XLA Ops:
  0.6 6.4 %copy.61 = f32[4,96,32,128]{3,1,2,0:T(8,128)S(1)} copy(f32[4,96,32,128]{3,2,1,0:T(8,128)} %param.4) | data formatting | bytes 12582912 | tf_op args[0]
  7.1 1.3 fusion.23
  8.4 2.3 collective-permute-start.1
  10.7 3.6 %collective-permute-start = (f32[1,96,32,128]{3,1,2,0:T(8,128)}, f32[1,96,32,128]{3,1,2,0:T(8,128)}, u32[]{:S(2)}, u32[]{:S(2)}) collective-permute-start(f32[1,96,32,128]{3,1,2,0:T(8,128)} %get-tuple-element.33), channel_id=1, source_target_pairs={{16,0},{32,16},{48,32},{64,48},{80,64},{96,80},{112,96},{17,1},{33... | collective-permute-start | bytes 4718600 | tf_op jit(solution)/shard_map/ppermute | solution.py:18
  14.4 2.4 collective-permute-start.2
  16.8 3.5 %collective-permute-start.3 = (f32[4,1,32,128]{3,1,2,0:T(1,128)S(1)}, f32[4,1,32,128]{3,1,2,0:T(1,128)S(1)}, u32[]{:S(2)}, u32[]{:S(2)}) collective-permute-start(f32[4,1,32,128]{3,1,2,0:T(1,128)S(1)} %bitcast.14), channel_id=1, source_target_pairs={{0,4},{4,8},{8,12},{1,5},{5,9},{9,13},{2,6},{6,10},{10,14},{3,7},{... | collective-permute-start | bytes 196616 | tf_op jit(solution)/shard_map/ppermute | solution.py:17
  22.4 5.4 %collective-permute-start.5 = (f32[4,96,1,128]{3,1,2,0:T(8,128)}, f32[4,96,1,128]{3,1,2,0:T(8,128)}, u32[]{:S(2)}, u32[]{:S(2)}) collective-permute-start(f32[4,96,1,128]{3,1,2,0:T(8,128)} %get-tuple-element.29), channel_id=1, source_target_pairs={{0,1},{1,2},{2,3},{4,5},{5,6},{6,7},{8,9},{9,10},{10,11},{12,13},{... | collective-permute-start | bytes 589832 | tf_op jit(solution)/shard_map/ppermute | solution.py:17
  27.9 2.7 collective-permute-done.1
  33.1 6.8 %constant_dynamic-update-slice_fusion.1 = f32[6,96,32,128]{3,1,2,0:T(8,128)} fusion(f32[6,96,32,128]{3,1,2,0:T(8,128)} %constant_dynamic-update-slice_fusion.2, f32[4,96,32,128]{3,2,1,0:T(8,128)S(1)} %copy-done.2), kind=kLoop, calls=%fused_computation.89 | loop fusion | bytes 12582912
  39.9 2.9 %constant_dynamic-update-slice_fusion = f32[6,96,32,128]{3,1,2,0:T(8,128)} fusion(f32[6,96,32,128]{3,1,2,0:T(8,128)} %constant_dynamic-update-slice_fusion.1, f32[1,96,32,128]{3,1,2,0:T(8,128)} %collective-permute-done), kind=kLoop, calls=%fused_computation.88 | loop fusion | bytes 3145728 | tf_op jit(solution)/shard_map/concatenate | solution.py:24
  42.8 29.4 %multiply_add_fusion.3 = f32[4,96,32,128]{3,1,2,0:T(8,128)} fusion(f32[4,96,32,128]{3,1,2,0:T(8,128)} %copy-done.1, f32[4,96,1,128]{3,1,2,0:T(8,128)S(1)} %collective-permute-done.4, f32[6,1,32,128]{3,1,2,0:T(1,128)S(1)} %pad.50, f32[6,96,32,128]{3,1,2,0:T(8,128)} %constant_dynamic-update-slice_fusion, f32[6,1,32,128]{3,1,2,0:T(1,128)S(1)} %pad.51, ...), kind=kLoop, calls=%fused_computation.79 | loop fusion | flops 53477376 | bytes 44630016 | tf_op jit(solution)/shard_map/add | solution.py:66
  72.2 2.1 fusion.20
  74.3 1.9 collective-permute-start.6
  76.2 3.6 %collective-permute-start.7 = (f32[1,96,32,128]{3,1,2,0:T(8,128)S(1)}, f32[1,96,32,128]{3,1,2,0:T(8,128)}, u32[]{:S(2)}, u32[]{:S(2)}) collective-permute-start(f32[1,96,32,128]{3,1,2,0:T(8,128)S(1)} %get-tuple-element.27), channel_id=1, source_target_pairs={{0,16},{16,32},{32,48},{48,64},{64,80},{80,96},{96,112},{1,17},{17... | collective-permute-start | bytes 4718600 | tf_op jit(solution)/shard_map/ppermute | solution.py:17
  80.9 1.3 collective-permute-start.10
  82.2 4.6 %collective-permute-start.11 = (f32[4,96,1,128]{3,1,2,0:T(8,128)S(1)}, f32[4,96,1,128]{3,1,2,0:T(8,128)S(1)}, u32[]{:S(2)}, u32[]{:S(2)}) collective-permute-start(f32[4,96,1,128]{3,1,2,0:T(8,128)S(1)} %get-tuple-element.23), channel_id=1, source_target_pairs={{0,1},{1,2},{2,3},{4,5},{5,6},{6,7},{8,9},{9,10},{10,11},{12,13},{... | collective-permute-start | bytes 589832 | tf_op jit(solution)/shard_map/ppermute | solution.py:17
  86.7 1.3 fusion.19
  88.0 2.4 collective-permute-start.8
  90.4 3.8 %collective-permute-done.8 = f32[4,1,32,128]{3,1,2,0:T(1,128)S(1)} collective-permute-done((f32[4,1,32,128]{3,1,2,0:T(1,128)S(1)}, f32[4,1,32,128]{3,1,2,0:T(1,128)S(1)}, u32[]{:S(2)}, u32[]{:S(2)}) %collective-permute-start.8) | collective-permute-done | bytes 65568 | tf_op jit(solution)/shard_map/ppermute | solution.py:18
  94.2 3.7 %collective-permute-start.9 = (f32[4,1,32,128]{3,1,2,0:T(1,128)S(1)}, f32[4,1,32,128]{3,1,2,0:T(1,128)S(1)}, u32[]{:S(2)}, u32[]{:S(2)}) collective-permute-start(f32[4,1,32,128]{3,1,2,0:T(1,128)S(1)} %get-tuple-element.25), channel_id=1, source_target_pairs={{0,4},{4,8},{8,12},{1,5},{5,9},{9,13},{2,6},{6,10},{10,14},{3,7},{... | collective-permute-start | bytes 196616 | tf_op jit(solution)/shard_map/ppermute | solution.py:17
  98.0 2.4 collective-permute-done.9
  101.1 26.5 %multiply_add_fusion.2 = f32[4,96,32,128]{3,1,2,0:T(8,128)} fusion(f32[4,96,32,128]{3,1,2,0:T(8,128)} %multiply_add_fusion.3, f32[4,96,1,128]{3,1,2,0:T(8,128)S(1)} %collective-permute-done.10, f32[6,1,32,128]{3,1,2,0:T(1,128)S(1)} %pad.54, f32[1,96,32,128]{3,1,2,0:T(8,128)} %collective-permute-done.6, f32[1,96,32,128]{3,1,2,0:T(8,128)} %collective-permute-done.7, ...), kind=kLoop, calls=%fused_computation.78 | loop fusion | flops 66060288 | bytes 35192832 | tf_op jit(solution)/shard_map/add | solution.py:66
  127.6 2.1 fusion.17
  129.7 1.9 collective-permute-start.12
  131.6 3.6 %collective-permute-start.13 = (f32[1,96,32,128]{3,1,2,0:T(8,128)S(1)}, f32[1,96,32,128]{3,1,2,0:T(8,128)}, u32[]{:S(2)}, u32[]{:S(2)}) collective-permute-start(f32[1,96,32,128]{3,1,2,0:T(8,128)S(1)} %get-tuple-element.21), channel_id=1, source_target_pairs={{0,16},{16,32},{32,48},{48,64},{64,80},{80,96},{96,112},{1,17},{17... | collective-permute-start | bytes 4718600 | tf_op jit(solution)/shard_map/ppermute | solution.py:17
  136.2 1.3 collective-permute-start.16
  137.5 4.6 %collective-permute-start.17 = (f32[4,96,1,128]{3,1,2,0:T(8,128)S(1)}, f32[4,96,1,128]{3,1,2,0:T(8,128)S(1)}, u32[]{:S(2)}, u32[]{:S(2)}) collective-permute-start(f32[4,96,1,128]{3,1,2,0:T(8,128)S(1)} %get-tuple-element.17), channel_id=1, source_target_pairs={{0,1},{1,2},{2,3},{4,5},{5,6},{6,7},{8,9},{9,10},{10,11},{12,13},{... | collective-permute-start | bytes 589832 | tf_op jit(solution)/shard_map/ppermute | solution.py:17
  142.1 1.3 fusion.16
  143.4 1.9 collective-permute-start.14
  145.3 4.2 %collective-permute-done.14 = f32[4,1,32,128]{3,1,2,0:T(1,128)S(1)} collective-permute-done((f32[4,1,32,128]{3,1,2,0:T(1,128)S(1)}, f32[4,1,32,128]{3,1,2,0:T(1,128)S(1)}, u32[]{:S(2)}, u32[]{:S(2)}) %collective-permute-start.14) | collective-permute-done | bytes 65568 | tf_op jit(solution)/shard_map/ppermute | solution.py:18
  149.6 3.5 %collective-permute-start.15 = (f32[4,1,32,128]{3,1,2,0:T(1,128)S(1)}, f32[4,1,32,128]{3,1,2,0:T(1,128)S(1)}, u32[]{:S(2)}, u32[]{:S(2)}) collective-permute-start(f32[4,1,32,128]{3,1,2,0:T(1,128)S(1)} %get-tuple-element.19), channel_id=1, source_target_pairs={{0,4},{4,8},{8,12},{1,5},{5,9},{9,13},{2,6},{6,10},{10,14},{3,7},{... | collective-permute-start | bytes 196616 | tf_op jit(solution)/shard_map/ppermute | solution.py:17
  153.1 2.6 collective-permute-done.15
  156.5 25.8 %multiply_add_fusion.1 = f32[4,96,32,128]{3,1,2,0:T(8,128)} fusion(f32[4,96,32,128]{3,1,2,0:T(8,128)} %multiply_add_fusion.2, f32[4,96,1,128]{3,1,2,0:T(8,128)S(1)} %collective-permute-done.16, f32[6,1,32,128]{3,1,2,0:T(1,128)S(1)} %pad.58, f32[1,96,32,128]{3,1,2,0:T(8,128)} %collective-permute-done.12, f32[1,96,32,128]{3,1,2,0:T(8,128)} %collective-permute-done.13, ...), kind=kLoop, calls=%fused_computation.77 | loop fusion | flops 66060288 | bytes 35192832 | tf_op jit(solution)/shard_map/add | solution.py:66
  182.3 2.1 fusion.14
  184.4 1.9 collective-permute-start.18
  186.3 3.6 %collective-permute-start.19 = (f32[1,96,32,128]{3,1,2,0:T(8,128)S(1)}, f32[1,96,32,128]{3,1,2,0:T(8,128)}, u32[]{:S(2)}, u32[]{:S(2)}) collective-permute-start(f32[1,96,32,128]{3,1,2,0:T(8,128)S(1)} %get-tuple-element.15), channel_id=1, source_target_pairs={{0,16},{16,32},{32,48},{48,64},{64,80},{80,96},{96,112},{1,17},{17... | collective-permute-start | bytes 4718600 | tf_op jit(solution)/shard_map/ppermute | solution.py:17
  190.9 1.3 collective-permute-start.22
  192.2 4.6 %collective-permute-start.23 = (f32[4,96,1,128]{3,1,2,0:T(8,128)S(1)}, f32[4,96,1,128]{3,1,2,0:T(8,128)S(1)}, u32[]{:S(2)}, u32[]{:S(2)}) collective-permute-start(f32[4,96,1,128]{3,1,2,0:T(8,128)S(1)} %get-tuple-element.12), channel_id=1, source_target_pairs={{0,1},{1,2},{2,3},{4,5},{5,6},{6,7},{8,9},{9,10},{10,11},{12,13},{... | collective-permute-start | bytes 589832 | tf_op jit(solution)/shard_map/ppermute | solution.py:17
  196.8 1.3 fusion.13
  198.1 1.9 collective-permute-start.20
  200.0 4.2 %collective-permute-done.20 = f32[4,1,32,128]{3,1,2,0:T(1,128)S(1)} collective-permute-done((f32[4,1,32,128]{3,1,2,0:T(1,128)S(1)}, f32[4,1,32,128]{3,1,2,0:T(1,128)S(1)}, u32[]{:S(2)}, u32[]{:S(2)}) %collective-permute-start.20) | collective-permute-done | bytes 65568 | tf_op jit(solution)/shard_map/ppermute | solution.py:18
  204.3 3.7 %collective-permute-start.21 = (f32[4,1,32,128]{3,1,2,0:T(1,128)S(1)}, f32[4,1,32,128]{3,1,2,0:T(1,128)S(1)}, u32[]{:S(2)}, u32[]{:S(2)}) collective-permute-start(f32[4,1,32,128]{3,1,2,0:T(1,128)S(1)} %get-tuple-element.13), channel_id=1, source_target_pairs={{0,4},{4,8},{8,12},{1,5},{5,9},{9,13},{2,6},{6,10},{10,14},{3,7},{... | collective-permute-start | bytes 196616 | tf_op jit(solution)/shard_map/ppermute | solution.py:17
  208.1 2.3 collective-permute-done.21
  211.2 31.1 %add_reduce_fusion = (f32[4,32,128]{2,1,0:T(8,128)S(1)}, f32[4,32,128]{2,1,0:T(8,128)S(1)}, f32[4,96,32,128]{3,1,2,0:T(8,128)}) fusion(f32[4,96,32,128]{3,1,2,0:T(8,128)} %multiply_add_fusion.1, f32[6,1,32,128]{3,1,2,0:T(1,128)S(1)} %pad.62, f32[1,96,32,128]{3,1,2,0:T(8,128)} %collective-permute-done.18, f32[1,96,32,128]{3,1,2,0:T(8,128)} %collective-permute-done.19, ...), kind=kLoop, calls=%fused_computation.80 | loop fusion | flops 72318976 | bytes 35323904 | tf_op jit(solution)/shard_map/reduce_sum | solution.py:84
  243.4 4.9 %all-to-all-start = ((f32[4,1,32768]{2,1,0:T(1,128)}), f32[4,1,32768]{2,1,0:T(1,128)S(1)}, u32[]{:S(2)}, u32[]{:S(2)}) async-start(f32[4,1,32768]{2,1,0:T(1,128)} %broadcast_in_dim.3), calls=%async_computation | async-start | bytes 1048576 | tf_op jit(solution)/shard_map/all_to_all | solution.py:31
  248.3 9.1 %copy.81 = f32[4,96,32,128]{3,2,1,0:T(8,128)} copy(f32[4,96,32,128]{3,1,2,0:T(8,128)} %get-tuple-element.10) | data formatting | bytes 12582912
  258.0 4.0 %subtract_multiply_fusion = f32[4,96,32,128]{3,1,2,0:T(8,128)S(1)} fusion(f32[4,96,32,128]{3,1,2,0:T(8,128)} %get-tuple-element.10, f32[4,32,128]{2,1,0:T(8,128)S(1)} %bitcast.13, f32[4,32,128]{2,1,0:T(8,128)S(1)} %bitcast.12), kind=kLoop, calls=%fused_computation.74 | loop fusion | flops 3145728 | bytes 12713984 | tf_op jit(solution)/shard_map/mul | solution.py:92
  262.0 6.3 %copy.80 = f32[4,96,32,128]{3,2,1,0:T(8,128)} copy(f32[4,96,32,128]{3,1,2,0:T(8,128)S(1)} %subtract_multiply_fusion) | data formatting | bytes 12582912
  (63 shorter events, 11.9 us)
Async XLA Ops:
  7.1 32.9 %copy-start.1 = (f32[4,96,32,128]{3,1,2,0:T(8,128)}, f32[4,96,32,128]{3,1,2,0:T(8,128)S(1)}, u32[]{:S(2)}) copy-start(f32[4,96,32,128]{3,1,2,0:T(8,128)S(1)} %copy.61) | copy-start | bytes 18874372
  7.1 7.3 %copy-start.2 = (f32[4,96,32,128]{3,2,1,0:T(8,128)S(1)}, f32[4,96,32,128]{3,2,1,0:T(8,128)}, u32[]{:S(2)}) copy-start(f32[4,96,32,128]{3,2,1,0:T(8,128)} %param.4) | copy-start | bytes 18874372
  8.4 22.1 %collective-permute-start.1 = (f32[1,96,32,128]{3,1,2,0:T(8,128)S(1)}, f32[1,96,32,128]{3,1,2,0:T(8,128)S(1)}, u32[]{:S(2)}, u32[]{:S(2)}) collective-permute-start(f32[1,96,32,128]{3,1,2,0:T(8,128)S(1)} %get-tuple-element.34), channel_id=1, source_target_pairs={{0,16},{16,32},{32,48},{48,64},{64,80},{80,96},{96,112},{1,17},{17... | collective-permute-start | bytes 4718600 | tf_op jit(solution)/shard_map/ppermute | solution.py:17
  10.7 29.2 %collective-permute-start = (f32[1,96,32,128]{3,1,2,0:T(8,128)}, f32[1,96,32,128]{3,1,2,0:T(8,128)}, u32[]{:S(2)}, u32[]{:S(2)}) collective-permute-start(f32[1,96,32,128]{3,1,2,0:T(8,128)} %get-tuple-element.33), channel_id=1, source_target_pairs={{16,0},{32,16},{48,32},{64,48},{80,64},{96,80},{112,96},{17,1},{33... | collective-permute-start | bytes 4718600 | tf_op jit(solution)/shard_map/ppermute | solution.py:18
  14.4 7.9 %collective-permute-start.2 = (f32[4,1,32,128]{3,1,2,0:T(1,128)S(1)}, f32[4,1,32,128]{3,1,2,0:T(1,128)S(1)}, u32[]{:S(2)}, u32[]{:S(2)}) collective-permute-start(f32[4,1,32,128]{3,1,2,0:T(1,128)S(1)} %bitcast.15), channel_id=1, source_target_pairs={{4,0},{8,4},{12,8},{5,1},{9,5},{13,9},{6,2},{10,6},{14,10},{7,3},{... | collective-permute-start | bytes 196616 | tf_op jit(solution)/shard_map/ppermute | solution.py:18
  16.8 11.0 %collective-permute-start.3 = (f32[4,1,32,128]{3,1,2,0:T(1,128)S(1)}, f32[4,1,32,128]{3,1,2,0:T(1,128)S(1)}, u32[]{:S(2)}, u32[]{:S(2)}) collective-permute-start(f32[4,1,32,128]{3,1,2,0:T(1,128)S(1)} %bitcast.14), channel_id=1, source_target_pairs={{0,4},{4,8},{8,12},{1,5},{5,9},{9,13},{2,6},{6,10},{10,14},{3,7},{... | collective-permute-start | bytes 196616 | tf_op jit(solution)/shard_map/ppermute | solution.py:17
  21.1 21.7 %collective-permute-start.4 = (f32[4,96,1,128]{3,1,2,0:T(8,128)}, f32[4,96,1,128]{3,1,2,0:T(8,128)S(1)}, u32[]{:S(2)}, u32[]{:S(2)}) collective-permute-start(f32[4,96,1,128]{3,1,2,0:T(8,128)} %get-tuple-element.30), channel_id=1, source_target_pairs={{1,0},{2,1},{3,2},{5,4},{6,5},{7,6},{9,8},{10,9},{11,10},{13,12},{... | collective-permute-start | bytes 589832 | tf_op jit(solution)/shard_map/ppermute | solution.py:18
  22.4 20.4 %collective-permute-start.5 = (f32[4,96,1,128]{3,1,2,0:T(8,128)}, f32[4,96,1,128]{3,1,2,0:T(8,128)}, u32[]{:S(2)}, u32[]{:S(2)}) collective-permute-start(f32[4,96,1,128]{3,1,2,0:T(8,128)} %get-tuple-element.29), channel_id=1, source_target_pairs={{0,1},{1,2},{2,3},{4,5},{5,6},{6,7},{8,9},{9,10},{10,11},{12,13},{... | collective-permute-start | bytes 589832 | tf_op jit(solution)/shard_map/ppermute | solution.py:17
  30.5 1.2 copy-start.3
  31.8 11.0 %slice-start = ((s8[6291456]{0:T(1024)(128)(4,1)}), s8[4194304]{0:T(1024)(128)(4,1)S(1)}, s32[]{:S(2)}) async-start(s8[6291456]{0:T(1024)(128)(4,1)} %bitcast.6), calls=%async_computation.1 | async-start | bytes 8388608
  31.8 11.0 %slice-start.2 = ((s8[6291456]{0:T(1024)(128)(4,1)}), s8[4194304]{0:T(1024)(128)(4,1)S(1)}, s32[]{:S(2)}) async-start(s8[6291456]{0:T(1024)(128)(4,1)} %bitcast.8), calls=%async_computation.3 | async-start | bytes 8388608
  33.1 9.7 %slice-start.1 = ((s8[6291456]{0:T(1024)(128)(4,1)}), s8[2097152]{0:T(1024)(128)(4,1)S(1)}, s32[]{:S(2)}) async-start(s8[6291456]{0:T(1024)(128)(4,1)} %bitcast.6), calls=%async_computation.2 | async-start | bytes 4194304
  33.1 9.7 %slice-start.3 = ((s8[6291456]{0:T(1024)(128)(4,1)}), s8[2097152]{0:T(1024)(128)(4,1)S(1)}, s32[]{:S(2)}) async-start(s8[6291456]{0:T(1024)(128)(4,1)} %bitcast.8), calls=%async_computation.4 | async-start | bytes 4194304
  33.1 9.7 %copy-start = (f32[4,96,32,128]{3,2,1,0:T(8,128)S(1)}, f32[4,96,32,128]{3,2,1,0:T(8,128)}, u32[]{:S(2)}) copy-start(f32[4,96,32,128]{3,2,1,0:T(8,128)} %param.5) | copy-start | bytes 18874372
  74.3 26.1 %collective-permute-start.6 = (f32[1,96,32,128]{3,1,2,0:T(8,128)S(1)}, f32[1,96,32,128]{3,1,2,0:T(8,128)}, u32[]{:S(2)}, u32[]{:S(2)}) collective-permute-start(f32[1,96,32,128]{3,1,2,0:T(8,128)S(1)} %get-tuple-element.28), channel_id=1, source_target_pairs={{16,0},{32,16},{48,32},{64,48},{80,64},{96,80},{112,96},{17,1},{33... | collective-permute-start | bytes 4718600 | tf_op jit(solution)/shard_map/ppermute | solution.py:18
  76.2 24.9 %collective-permute-start.7 = (f32[1,96,32,128]{3,1,2,0:T(8,128)S(1)}, f32[1,96,32,128]{3,1,2,0:T(8,128)}, u32[]{:S(2)}, u32[]{:S(2)}) collective-permute-start(f32[1,96,32,128]{3,1,2,0:T(8,128)S(1)} %get-tuple-element.27), channel_id=1, source_target_pairs={{0,16},{16,32},{32,48},{48,64},{64,80},{80,96},{96,112},{1,17},{17... | collective-permute-start | bytes 4718600 | tf_op jit(solution)/shard_map/ppermute | solution.py:17
  80.9 19.5 %collective-permute-start.10 = (f32[4,96,1,128]{3,1,2,0:T(8,128)S(1)}, f32[4,96,1,128]{3,1,2,0:T(8,128)S(1)}, u32[]{:S(2)}, u32[]{:S(2)}) collective-permute-start(f32[4,96,1,128]{3,1,2,0:T(8,128)S(1)} %get-tuple-element.24), channel_id=1, source_target_pairs={{1,0},{2,1},{3,2},{5,4},{6,5},{7,6},{9,8},{10,9},{11,10},{13,12},{... | collective-permute-start | bytes 589832 | tf_op jit(solution)/shard_map/ppermute | solution.py:18
  82.2 18.3 %collective-permute-start.11 = (f32[4,96,1,128]{3,1,2,0:T(8,128)S(1)}, f32[4,96,1,128]{3,1,2,0:T(8,128)S(1)}, u32[]{:S(2)}, u32[]{:S(2)}) collective-permute-start(f32[4,96,1,128]{3,1,2,0:T(8,128)S(1)} %get-tuple-element.23), channel_id=1, source_target_pairs={{0,1},{1,2},{2,3},{4,5},{5,6},{6,7},{8,9},{9,10},{10,11},{12,13},{... | collective-permute-start | bytes 589832 | tf_op jit(solution)/shard_map/ppermute | solution.py:17
  88.0 6.2 %collective-permute-start.8 = (f32[4,1,32,128]{3,1,2,0:T(1,128)S(1)}, f32[4,1,32,128]{3,1,2,0:T(1,128)S(1)}, u32[]{:S(2)}, u32[]{:S(2)}) collective-permute-start(f32[4,1,32,128]{3,1,2,0:T(1,128)S(1)} %get-tuple-element.26), channel_id=1, source_target_pairs={{4,0},{8,4},{12,8},{5,1},{9,5},{13,9},{6,2},{10,6},{14,10},{7,3},{... | collective-permute-start | bytes 196616 | tf_op jit(solution)/shard_map/ppermute | solution.py:18
  94.2 6.1 %collective-permute-start.9 = (f32[4,1,32,128]{3,1,2,0:T(1,128)S(1)}, f32[4,1,32,128]{3,1,2,0:T(1,128)S(1)}, u32[]{:S(2)}, u32[]{:S(2)}) collective-permute-start(f32[4,1,32,128]{3,1,2,0:T(1,128)S(1)} %get-tuple-element.25), channel_id=1, source_target_pairs={{0,4},{4,8},{8,12},{1,5},{5,9},{9,13},{2,6},{6,10},{10,14},{3,7},{... | collective-permute-start | bytes 196616 | tf_op jit(solution)/shard_map/ppermute | solution.py:17
  100.4 0.7 copy-start.6
  129.7 26.1 %collective-permute-start.12 = (f32[1,96,32,128]{3,1,2,0:T(8,128)S(1)}, f32[1,96,32,128]{3,1,2,0:T(8,128)}, u32[]{:S(2)}, u32[]{:S(2)}) collective-permute-start(f32[1,96,32,128]{3,1,2,0:T(8,128)S(1)} %get-tuple-element.22), channel_id=1, source_target_pairs={{16,0},{32,16},{48,32},{64,48},{80,64},{96,80},{112,96},{17,1},{33... | collective-permute-start | bytes 4718600 | tf_op jit(solution)/shard_map/ppermute | solution.py:18
  131.6 24.9 %collective-permute-start.13 = (f32[1,96,32,128]{3,1,2,0:T(8,128)S(1)}, f32[1,96,32,128]{3,1,2,0:T(8,128)}, u32[]{:S(2)}, u32[]{:S(2)}) collective-permute-start(f32[1,96,32,128]{3,1,2,0:T(8,128)S(1)} %get-tuple-element.21), channel_id=1, source_target_pairs={{0,16},{16,32},{32,48},{48,64},{64,80},{80,96},{96,112},{1,17},{17... | collective-permute-start | bytes 4718600 | tf_op jit(solution)/shard_map/ppermute | solution.py:17
  136.2 19.5 %collective-permute-start.16 = (f32[4,96,1,128]{3,1,2,0:T(8,128)S(1)}, f32[4,96,1,128]{3,1,2,0:T(8,128)S(1)}, u32[]{:S(2)}, u32[]{:S(2)}) collective-permute-start(f32[4,96,1,128]{3,1,2,0:T(8,128)S(1)} %get-tuple-element.18), channel_id=1, source_target_pairs={{1,0},{2,1},{3,2},{5,4},{6,5},{7,6},{9,8},{10,9},{11,10},{13,12},{... | collective-permute-start | bytes 589832 | tf_op jit(solution)/shard_map/ppermute | solution.py:18
  137.5 18.3 %collective-permute-start.17 = (f32[4,96,1,128]{3,1,2,0:T(8,128)S(1)}, f32[4,96,1,128]{3,1,2,0:T(8,128)S(1)}, u32[]{:S(2)}, u32[]{:S(2)}) collective-permute-start(f32[4,96,1,128]{3,1,2,0:T(8,128)S(1)} %get-tuple-element.17), channel_id=1, source_target_pairs={{0,1},{1,2},{2,3},{4,5},{5,6},{6,7},{8,9},{9,10},{10,11},{12,13},{... | collective-permute-start | bytes 589832 | tf_op jit(solution)/shard_map/ppermute | solution.py:17
  143.4 6.2 %collective-permute-start.14 = (f32[4,1,32,128]{3,1,2,0:T(1,128)S(1)}, f32[4,1,32,128]{3,1,2,0:T(1,128)S(1)}, u32[]{:S(2)}, u32[]{:S(2)}) collective-permute-start(f32[4,1,32,128]{3,1,2,0:T(1,128)S(1)} %get-tuple-element.20), channel_id=1, source_target_pairs={{4,0},{8,4},{12,8},{5,1},{9,5},{13,9},{6,2},{10,6},{14,10},{7,3},{... | collective-permute-start | bytes 196616 | tf_op jit(solution)/shard_map/ppermute | solution.py:18
  149.6 6.1 %collective-permute-start.15 = (f32[4,1,32,128]{3,1,2,0:T(1,128)S(1)}, f32[4,1,32,128]{3,1,2,0:T(1,128)S(1)}, u32[]{:S(2)}, u32[]{:S(2)}) collective-permute-start(f32[4,1,32,128]{3,1,2,0:T(1,128)S(1)} %get-tuple-element.19), channel_id=1, source_target_pairs={{0,4},{4,8},{8,12},{1,5},{5,9},{9,13},{2,6},{6,10},{10,14},{3,7},{... | collective-permute-start | bytes 196616 | tf_op jit(solution)/shard_map/ppermute | solution.py:17
  155.8 0.7 copy-start.7
  184.4 26.2 %collective-permute-start.18 = (f32[1,96,32,128]{3,1,2,0:T(8,128)S(1)}, f32[1,96,32,128]{3,1,2,0:T(8,128)}, u32[]{:S(2)}, u32[]{:S(2)}) collective-permute-start(f32[1,96,32,128]{3,1,2,0:T(8,128)S(1)} %get-tuple-element.16), channel_id=1, source_target_pairs={{16,0},{32,16},{48,32},{64,48},{80,64},{96,80},{112,96},{17,1},{33... | collective-permute-start | bytes 4718600 | tf_op jit(solution)/shard_map/ppermute | solution.py:18
  186.3 24.9 %collective-permute-start.19 = (f32[1,96,32,128]{3,1,2,0:T(8,128)S(1)}, f32[1,96,32,128]{3,1,2,0:T(8,128)}, u32[]{:S(2)}, u32[]{:S(2)}) collective-permute-start(f32[1,96,32,128]{3,1,2,0:T(8,128)S(1)} %get-tuple-element.15), channel_id=1, source_target_pairs={{0,16},{16,32},{32,48},{48,64},{64,80},{80,96},{96,112},{1,17},{17... | collective-permute-start | bytes 4718600 | tf_op jit(solution)/shard_map/ppermute | solution.py:17
  190.9 19.5 %collective-permute-start.22 = (f32[4,96,1,128]{3,1,2,0:T(8,128)S(1)}, f32[4,96,1,128]{3,1,2,0:T(8,128)S(1)}, u32[]{:S(2)}, u32[]{:S(2)}) collective-permute-start(f32[4,96,1,128]{3,1,2,0:T(8,128)S(1)} %get-tuple-element.11), channel_id=1, source_target_pairs={{1,0},{2,1},{3,2},{5,4},{6,5},{7,6},{9,8},{10,9},{11,10},{13,12},{... | collective-permute-start | bytes 589832 | tf_op jit(solution)/shard_map/ppermute | solution.py:18
  192.2 18.3 %collective-permute-start.23 = (f32[4,96,1,128]{3,1,2,0:T(8,128)S(1)}, f32[4,96,1,128]{3,1,2,0:T(8,128)S(1)}, u32[]{:S(2)}, u32[]{:S(2)}) collective-permute-start(f32[4,96,1,128]{3,1,2,0:T(8,128)S(1)} %get-tuple-element.12), channel_id=1, source_target_pairs={{0,1},{1,2},{2,3},{4,5},{5,6},{6,7},{8,9},{9,10},{10,11},{12,13},{... | collective-permute-start | bytes 589832 | tf_op jit(solution)/shard_map/ppermute | solution.py:17
  198.1 6.2 %collective-permute-start.20 = (f32[4,1,32,128]{3,1,2,0:T(1,128)S(1)}, f32[4,1,32,128]{3,1,2,0:T(1,128)S(1)}, u32[]{:S(2)}, u32[]{:S(2)}) collective-permute-start(f32[4,1,32,128]{3,1,2,0:T(1,128)S(1)} %get-tuple-element.14), channel_id=1, source_target_pairs={{4,0},{8,4},{12,8},{5,1},{9,5},{13,9},{6,2},{10,6},{14,10},{7,3},{... | collective-permute-start | bytes 196616 | tf_op jit(solution)/shard_map/ppermute | solution.py:18
  204.3 6.1 %collective-permute-start.21 = (f32[4,1,32,128]{3,1,2,0:T(1,128)S(1)}, f32[4,1,32,128]{3,1,2,0:T(1,128)S(1)}, u32[]{:S(2)}, u32[]{:S(2)}) collective-permute-start(f32[4,1,32,128]{3,1,2,0:T(1,128)S(1)} %get-tuple-element.13), channel_id=1, source_target_pairs={{0,4},{4,8},{8,12},{1,5},{5,9},{9,13},{2,6},{6,10},{10,14},{3,7},{... | collective-permute-start | bytes 196616 | tf_op jit(solution)/shard_map/ppermute | solution.py:17
  210.5 0.7 copy-start.4
  210.5 0.7 copy-start.5
  243.4 14.0 %all-to-all-start = ((f32[4,1,32768]{2,1,0:T(1,128)}), f32[4,1,32768]{2,1,0:T(1,128)S(1)}, u32[]{:S(2)}, u32[]{:S(2)}) async-start(f32[4,1,32768]{2,1,0:T(1,128)} %broadcast_in_dim.3), calls=%async_computation | async-start | bytes 1048576 | tf_op jit(solution)/shard_map/all_to_all | solution.py:31
where the time goes:
time: 274 us; the launch traced here: 269 us
  other arithmetic  117 us (43%)
  starting transfers between devices  74.5 us (27%)
  local copies, waits for them, and re-layouts  53.2 us (19%)
  waiting for transfers between devices  22.3 us (8%)
    add x3, other arithmetic, march_one_step(): middle - scaled_wind_north * slopes[0] - scaled_wind_east * slopes[1]  81.6 us
    ppermute x12, starting transfers between devices, padded(): lax.ppermute(last, axis, up)  46.4 us
    unnamed x29, local copies, waits for them, and re-layouts  33.3 us
    reduce_sum x1, other arithmetic, shards(): jnp.sum(moved, axis=1, keepdims=True)  31.1 us
    ppermute x12, starting transfers between devices, padded(): lax.ppermute(initial, axis, [(b, a) for a, b in up])  23.1 us
    slice x10, local copies, waits for them, and re-layouts, padded(): last = lax.slice_in_dim(array, length - width, length, axis=dim)  13.1 us
    ppermute x12, waiting for transfers between devices, padded(): lax.ppermute(initial, axis, [(b, a) for a, b in up])  12.3 us
    ppermute x12, waiting for transfers between devices, padded(): lax.ppermute(last, axis, up)  10 us
  transfers between devices with their start and end apart: 25, of which 7 were waited for; matrix products, arithmetic and copies ran while one was open for 11% of the time, Pallas kernels for 0%

commit v1 on v0

v1 whole, which is shorter than its diff:
```python
import functools

import jax
import jax.numpy as jnp
from jax import lax
from jax.experimental import pallas as pl
from jax.experimental.pallas import tpu as pltpu
from jax.sharding import PartitionSpec as P

STEPS = 4
CHUNKS = 4
UNROLL = 8
MESH = pl.DeviceIdType.MESH


def march(cur, ahead, behind, east, west, above, below, wind_n, wind_e, wind_u, sign):
    spread = ahead + behind + east + west + above + below
    new = 0.7 * cur + 0.05 * spread
    new = new - (sign * wind_n) * (ahead - behind)
    new = new - wind_e * (east - west)
    return new - wind_u * (above - below)


def advance(
    state, north, east, upward, end, stats,
    field, winds, face, halo, mine, theirs,
    load_sem, slow_s, slow_r, fast_s, fast_r, lon_s, lon_r, lev_s, lev_r, stat_s, stat_r,
):
    planes, length, depth, members = state.shape
    lat, lon, lev = (lax.axis_index(a) for a in ("lat", "lon", "lev"))
    n_lat, n_lon, n_lev = (lax.axis_size(a) for a in ("lat", "lon", "lev"))
    core = lax.rem(lat, 2)
    way = 2 * core - 1
    sign = way.astype(jnp.float32)
    slow, fast = lat + way, lat - way
    last = planes - 1
    part = length // CHUNKS

    def row(q):
        return core * q + (1 - core) * (last - q)

    def slot(t, q):
        if q < 0:
            return 2 * planes + 2 * t + 1
        if q > last:
            return 2 * planes + 2 * t
        return planes * (t % 2) + q

    has_slow = jnp.logical_and(slow >= 0, slow < n_lat)
    has_lon = (lon > 0, lon < n_lon - 1)
    has_lev = (lev > 0, lev < n_lev - 1)

    def load(k, q):
        ref = (state, north, east, upward)[k]
        dst = field.at[slot(0, q), pl.ds(1, length)] if k == 0 else winds.at[k - 1, q]
        return pltpu.make_async_copy(ref.at[row(q)], dst, load_sem.at[k, q])

    order = [last, *range(last)]
    for q in order:
        load(0, q).start()
    for q in [*range(last), last]:
        for k in (1, 2, 3):
            load(k, q).start()

    barrier = pltpu.get_barrier_semaphore()

    def greet(**there):
        pl.semaphore_signal(barrier, inc=1, device_id=there, device_id_type=MESH)

    greet(lat=fast)
    pl.when(has_slow)(lambda: greet(lat=slow))
    for d in range(1, n_lon):
        greet(lon=lax.rem(lon + d, n_lon))
    pl.when(has_lev[0])(lambda: greet(lev=lev - 1))
    pl.when(has_lev[1])(lambda: greet(lev=lev + 1))
    count = n_lon + sum(h.astype(jnp.int32) for h in (has_slow, *has_lev))
    pl.semaphore_wait(barrier, count)

    def to_slow(t, c):
        xs = pl.ds(1 + c * part, part)
        return pltpu.make_async_remote_copy(
            field.at[slot(t, last), xs], field.at[slot(t, planes), xs],
            slow_s.at[t, c], slow_r.at[t, c], device_id={"lat": slow}, device_id_type=MESH,
        )

    def to_fast(t):
        xs = pl.ds(1, length)
        return pltpu.make_async_remote_copy(
            field.at[slot(t, 0), xs], field.at[slot(t, -1), xs],
            fast_s.at[t], fast_r.at[t], device_id={"lat": fast}, device_id_type=MESH,
        )

    groups = (pl.ds(0, last), pl.ds(last, 1))
    slots = lambda t, g: pl.ds(slot(t, 0), last) if g == 0 else pl.ds(slot(t, last), 1)

    def to_lon(t, side, g):
        src, dst = (1, length + 1) if side == 0 else (length, 0)
        return pltpu.make_async_remote_copy(
            field.at[slots(t, g), src], field.at[slots(t, g), dst],
            lon_s.at[t, side, g], lon_r.at[t, side, g],
            device_id={"lon": lon - 1 if side == 0 else lon + 1}, device_id_type=MESH,
        )

    def to_lev(t, side, g):
        return pltpu.make_async_remote_copy(
            face.at[t, side, groups[g]], halo.at[t, 1 - side, groups[g]],
            lev_s.at[t, side, g], lev_r.at[t, side, g],
            device_id={"lev": lev - 1 if side == 0 else lev + 1}, device_id_type=MESH,
        )

    def to_stat(d, g):
        return pltpu.make_async_remote_copy(
            mine.at[groups[g]], theirs.at[n_lon - 1 - d, groups[g]],
            stat_s.at[g, d - 1], stat_r.at[g, n_lon - 1 - d],
            device_id={"lon": lax.rem(lon + d, n_lon)}, device_id_type=MESH,
        )

    def start_edges(t, g):
        for side in (0, 1):
            pl.when(has_lon[side])(lambda: to_lon(t, side, g).start())
            pl.when(has_lev[side])(lambda: to_lev(t, side, g).start())

    def wait_edges(t, g):
        for side in (0, 1):
            pl.when(has_lon[1 - side])(lambda: to_lon(t, side, g).wait_recv())
            pl.when(has_lev[1 - side])(lambda: to_lev(t, side, g).wait_recv())

    def wait_edges_sent(t, g):
        for side in (0, 1):
            pl.when(has_lon[side])(lambda: to_lon(t, side, g).wait_send())
            pl.when(has_lev[side])(lambda: to_lev(t, side, g).wait_send())

    def clear(ref, index, n):
        def body(i, _):
            ref[(*index, i)] = jnp.zeros(ref.shape[len(index) + 1 :], ref.dtype)
            return 0

        lax.fori_loop(0, n, body, 0)

    edge_rows = (0, length + 1)
    for side in (0, 1):

        @pl.when(jnp.logical_not(has_lon[side]))
        def _(side=side):
            for s in range(2 * planes):
                field[s, edge_rows[side]] = jnp.zeros((depth, members), jnp.float32)

        @pl.when(jnp.logical_not(has_lev[side]))
        def _(side=side):
            for t in range(STEPS):
                clear(halo, (t, side), planes)

    load(0, last).wait()
    for c in range(CHUNKS):
        pl.when(has_slow)(lambda: to_slow(0, c).start())
    load(0, 0).wait()
    to_fast(0).start()
    for q in range(1, last):
        load(0, q).wait()

    def pack(t, q):
        def body(i, _):
            for j in range(UNROLL):
                x = i * UNROLL + j
                face[t, 0, q, pl.ds(x, 1), :] = field[slot(t, q), 1 + x, pl.ds(0, 1), :]
                face[t, 1, q, pl.ds(x, 1), :] = field[slot(t, q), 1 + x, pl.ds(depth - 1, 1), :]
            return 0

        lax.fori_loop(0, length // UNROLL, body, 0)

    for q in range(planes):
        pack(0, q)
    for g in (0, 1):
        start_edges(0, g)

    @pl.when(jnp.logical_not(has_slow))
    def _():
        for t in range(STEPS):
            clear(field, (slot(t, planes),), length + 2)

    level = lax.broadcasted_iota(jnp.int32, (depth, members), 0)

    def cells(t, q, x):
        here = slot(t, q)
        cur = field[here, x + 1]
        below = jnp.where(level == 0, halo[t, 0, q, pl.ds(x, 1), :], pltpu.roll(cur, 1, 0))
        above = jnp.where(
            level == depth - 1, halo[t, 1, q, pl.ds(x, 1), :], pltpu.roll(cur, depth - 1, 0)
        )
        return march(
            cur, field[slot(t, q + 1), x + 1], field[slot(t, q - 1), x + 1],
            field[here, x + 2], field[here, x], above, below,
            winds[0, q, x], winds[1, q, x], winds[2, q, x], sign,
        )

    def run(t, q, first, n):
        def body(i, _):
            for j in range(UNROLL):
                x = first + i * UNROLL + j
                new = cells(t, q, x)
                field[slot(t + 1, q), x + 1] = new
                face[t + 1, 0, q, pl.ds(x, 1), :] = new[:1]
                face[t + 1, 1, q, pl.ds(x, 1), :] = new[depth - 1 :]
            return 0

        lax.fori_loop(0, n // UNROLL, body, 0)

    def run_end(t, q, first, n, sums):
        guess = field[slot(t, q), length // 2]

        def body(i, sums):
            total, squares = sums
            for j in range(UNROLL):
                x = first + i * UNROLL + j
                new = cells(t, q, x)
                end[row(q), x] = new
                moved = new - guess
                total = total + moved
                squares = squares + moved * moved
            return total, squares

        return lax.fori_loop(0, n // UNROLL, body, sums)

    def summarise(t, q, sums):
        total, squares = sums
        guess = field[slot(t, q), length // 2]
        mean = total * (1.0 / length)
        mine[q, 0] = guess + mean
        mine[q, 1] = squares - total * mean

    zero = jnp.zeros((depth, members), jnp.float32)
    for t in range(STEPS):
        final = t == STEPS - 1
        if t > 0:
            to_fast(t - 1).wait_send()
        to_fast(t).wait_recv()
        for g in (0, 1):
            wait_edges(t, g)
            if t > 0:
                wait_edges_sent(t - 1, g)
        for q in range(last):
            if t == 0:
                for k in (1, 2, 3):
                    load(k, q).wait()
            if final:
                summarise(t, q, run_end(t, q, 0, length, (zero, zero)))
            else:
                run(t, q, 0, length)
                if q == 0:
                    to_fast(t + 1).start()
        if final:
            for d in range(1, n_lon):
                to_stat(d, 0).start()
        else:
            start_edges(t + 1, 0)
        if t == 0:
            for k in (1, 2, 3):
                load(k, last).wait()
        sums = (zero, zero)
        for c in range(CHUNKS):

            @pl.when(has_slow)
            def _(c=c):
                if t > 0:
                    to_slow(t - 1, c).wait_send()
                to_slow(t, c).wait_recv()

            if final:
                sums = run_end(t, last, c * part, part, sums)
            else:
                run(t, last, c * part, part)
                pl.when(has_slow)(lambda: to_slow(t + 1, c).start())
        if final:
            summarise(t, last, sums)
            for d in range(1, n_lon):
                to_stat(d, 1).start()
        else:
            start_edges(t + 1, 1)

    t = STEPS - 1
    for c in range(CHUNKS):
        pl.when(has_slow)(lambda: to_slow(t, c).wait_send())
    to_fast(t).wait_send()
    for g in (0, 1):
        wait_edges_sent(t, g)
    for g in (0, 1):
        for d in range(1, n_lon):
            to_stat(d, g).wait()
    for q in range(planes):
        means = [mine[q, 0], *(theirs[d, q, 0] for d in range(n_lon - 1))]
        parts = [mine[q, 1], *(theirs[d, q, 1] for d in range(n_lon - 1))]
        mean = sum(means) * (1.0 / n_lon)
        apart = sum((m - mean) * (m - mean) for m in means)
        variance = (sum(parts) + length * apart) * (1.0 / (length * n_lon))
        stats[row(q), 0] = mean
        stats[row(q), 1] = lax.rsqrt(variance + 0.0001)


def normalise(end, stats, normalised, final, scratch, sem):
    planes, length = end.shape[:2]
    copies = [pltpu.make_async_copy(end, final, sem.at[planes])]
    copies[0].start()
    for p in range(planes):
        mean, scale = stats[p, 0], stats[p, 1]

        def body(i, _, p=p, mean=mean, scale=scale):
            for j in range(UNROLL):
                x = i * UNROLL + j
                scratch[p, x] = (end[p, x] - mean) * scale
            return 0

        lax.fori_loop(0, length // UNROLL, body, 0)
        copies.append(pltpu.make_async_copy(scratch.at[p], normalised.at[p], sem.at[p]))
        copies[-1].start()
    for copy in copies:
        copy.wait()


def shards(initial_state, wind_north, wind_east, wind_upward):
    planes, length, depth, members = initial_state.shape
    n_lon = lax.axis_size("lon")
    block = initial_state.shape
    f32 = jnp.float32
    dma = pltpu.SemaphoreType.DMA
    anywhere = pl.BlockSpec(memory_space=pl.ANY)
    vmem = pl.BlockSpec(memory_space=pltpu.VMEM)
    end, stats = pl.pallas_call(
        advance,
        out_shape=(
            pltpu.VMEM(block, f32),
            pltpu.VMEM((planes, 2, depth, members), f32),
        ),
        in_specs=[anywhere] * 4,
        out_specs=(vmem, vmem),
        scratch_shapes=[
            pltpu.VMEM((2 * planes + 2 * STEPS, length + 2, depth, members), f32),
            pltpu.VMEM((3, *block), f32),
            pltpu.VMEM((STEPS, 2, planes, length, members), f32),
            pltpu.VMEM((STEPS, 2, planes, length, members), f32),
            pltpu.VMEM((planes, 2, depth, members), f32),
            pltpu.VMEM((n_lon - 1, planes, 2, depth, members), f32),
            dma((4, planes)),
            dma((STEPS, CHUNKS)), dma((STEPS, CHUNKS)),
            dma((STEPS,)), dma((STEPS,)),
            dma((STEPS, 2, 2)), dma((STEPS, 2, 2)),
            dma((STEPS, 2, 2)), dma((STEPS, 2, 2)),
            dma((2, n_lon - 1)), dma((2, n_lon - 1)),
        ],
        compiler_params=pltpu.CompilerParams(
            collective_id=0, has_side_effects=True, vmem_limit_bytes=54 * 1024 * 1024
        ),
        name="advance",
    )(initial_state, wind_north, wind_east, wind_upward)
    end, stats = (pltpu.with_memory_space_constraint(a, pltpu.VMEM) for a in (end, stats))
    return pl.pallas_call(
        normalise,
        out_shape=(jax.ShapeDtypeStruct(block, f32), jax.ShapeDtypeStruct(block, f32)),
        in_specs=[vmem, vmem],
        out_specs=(anywhere, anywhere),
        scratch_shapes=[pltpu.VMEM(block, f32), dma((planes + 1,))],
        compiler_params=pltpu.CompilerParams(vmem_limit_bytes=32 * 1024 * 1024),
        name="normalise",
    )(end, stats)


def solution(mesh):
    spec = P("lat", "lon", "lev", None)
    return jax.shard_map(
        shards, mesh=mesh, in_specs=(spec,) * 4, out_specs=(spec, spec), check_vma=False
    )
```

time: 274 us -> 85 us (0.31)
  the two profiles are of different devices: /device:TPU:14 before, /device:TPU:1 now
where the time goes in v1:
time: 85 us; the launch traced here: 84.9 us
  Pallas kernels  84.3 us (99%)
    pallas_call x1, Pallas kernels, shards(): pl.pallas_call(advance, out_shape=(pltpu.VMEM(block, f32), pltpu.VMEM((pl...  79.6 us
    pallas_call x1, Pallas kernels, shards(): pl.pallas_call(normalise, out_shape=(jax.ShapeDtypeStruct(block, f32), ja...  4.68 us

profile of v1, /device:TPU:1, one launch (start us, length us, event | category | flops | bytes accessed | tf_op | source)
XLA Modules:
  0.0 84.9 jit_solution(7346980246813698303)
XLA Ops:
  0.6 79.6 %advance.1 = (f32[4,96,32,128]{3,2,1,0:T(8,128)S(1)}, f32[4,2,32,128]{3,2,1,0:T(8,128)S(1)}) custom-call(f32[4,96,32,128]{3,2,1,0:T(8,128)} %state.1, f32[4,96,32,128]{3,2,1,0:T(8,128)} %north.1, f32[4,96,32,128]{3,2,1,0:T(8,128)} %east.1, f32[4,96,32,128]{3,2,1,0:T(8,128)} %upward.1), custom_call_target="tpu_custom_call" | custom-call | tf_op jit(solution)/shard_map/advance/pallas_call | solution.py:327
  80.2 4.7 %normalise.1 = (f32[4,96,32,128]{3,2,1,0:T(8,128)}, f32[4,96,32,128]{3,2,1,0:T(8,128)}) custom-call(f32[4,96,32,128]{3,2,1,0:T(8,128)S(1)} %get-tuple-element.4.end, f32[4,2,32,128]{3,2,1,0:T(8,128)S(1)} %get-tuple-element.5.stats), custom_call_target="tpu_custom_call" | custom-call | tf_op jit(solution)/shard_map/normalise/pallas_call | solution.py:355

commit v2 on v1

--- a/solution.py
+++ b/solution.py
@@ -10,6 +10,8 @@
 STEPS = 4
 CHUNKS = 4
 UNROLL = 8
+UNROLL_PIECE = 24
+PARTS = 2
 MESH = pl.DeviceIdType.MESH
 
 
@@ -24,7 +26,7 @@
 def advance(
     state, north, east, upward, end, stats,
     field, winds, face, halo, mine, theirs,
-    load_sem, slow_s, slow_r, fast_s, fast_r, lon_s, lon_r, lev_s, lev_r, stat_s, stat_r,
+    load_sem, piece_sem, slow_s, slow_r, fast_s, fast_r, lon_s, lon_r, lev_s, lev_r, stat_s, stat_r, above_sem,
 ):
     planes, length, depth, members = state.shape
     lat, lon, lev = (lax.axis_index(a) for a in ("lat", "lon", "lev"))
@@ -34,7 +36,7 @@
     sign = way.astype(jnp.float32)
     slow, fast = lat + way, lat - way
     last = planes - 1
-    part = length // CHUNKS
+    part = depth // CHUNKS
 
     def row(q):
         return core * q + (1 - core) * (last - q)
@@ -55,12 +57,15 @@
         dst = field.at[slot(0, q), pl.ds(1, length)] if k == 0 else winds.at[k - 1, q]
         return pltpu.make_async_copy(ref.at[row(q)], dst, load_sem.at[k, q])
 
-    order = [last, *range(last)]
-    for q in order:
-        load(0, q).start()
-    for q in [*range(last), last]:
-        for k in (1, 2, 3):
-            load(k, q).start()
+    def load_piece(c):
+        zs = pl.ds(c * part, part)
+        return pltpu.make_async_copy(
+            state.at[row(last), :, zs],
+            field.at[slot(0, last), pl.ds(1, length), zs],
+            piece_sem.at[c],
+        )
+
+    load_piece(0).start()
 
     barrier = pltpu.get_barrier_semaphore()
 
@@ -69,17 +74,24 @@
 
     greet(lat=fast)
     pl.when(has_slow)(lambda: greet(lat=slow))
-    for d in range(1, n_lon):
-        greet(lon=lax.rem(lon + d, n_lon))
-    pl.when(has_lev[0])(lambda: greet(lev=lev - 1))
+    pl.when(has_lon[1])(lambda: greet(lon=lon + 1))
     pl.when(has_lev[1])(lambda: greet(lev=lev + 1))
-    count = n_lon + sum(h.astype(jnp.int32) for h in (has_slow, *has_lev))
+    count = 1 + sum(h.astype(jnp.int32) for h in (has_slow, has_lon[0], has_lev[0]))
+    load_piece(0).wait()
+    for c in range(1, CHUNKS):
+        load_piece(c).start()
     pl.semaphore_wait(barrier, count)
 
+    def answer(**there):
+        pl.semaphore_signal(above_sem, inc=1, device_id=there, device_id_type=MESH)
+
+    pl.when(has_lon[0])(lambda: answer(lon=lon - 1))
+    pl.when(has_lev[0])(lambda: answer(lev=lev - 1))
+
     def to_slow(t, c):
-        xs = pl.ds(1 + c * part, part)
+        xs, zs = pl.ds(1, length), pl.ds(c * part, part)
         return pltpu.make_async_remote_copy(
-            field.at[slot(t, last), xs], field.at[slot(t, planes), xs],
+            field.at[slot(t, last), xs, zs], field.at[slot(t, planes), xs, zs],
             slow_s.at[t, c], slow_r.at[t, c], device_id={"lat": slow}, device_id_type=MESH,
         )
 
@@ -108,10 +120,11 @@
             device_id={"lev": lev - 1 if side == 0 else lev + 1}, device_id_type=MESH,
         )
 
-    def to_stat(d, g):
+    def to_stat(d, c):
+        where = (slice(0, last),) if c == CHUNKS else (last, slice(None), pl.ds(c * part, part))
         return pltpu.make_async_remote_copy(
-            mine.at[groups[g]], theirs.at[n_lon - 1 - d, groups[g]],
-            stat_s.at[g, d - 1], stat_r.at[g, n_lon - 1 - d],
+            mine.at[where], theirs.at[(n_lon - 1 - d, *where)],
+            stat_s.at[c, d - 1], stat_r.at[c, n_lon - 1 - d],
             device_id={"lon": lax.rem(lon + d, n_lon)}, device_id_type=MESH,
         )
 
@@ -130,6 +143,16 @@
             pl.when(has_lon[side])(lambda: to_lon(t, side, g).wait_send())
             pl.when(has_lev[side])(lambda: to_lev(t, side, g).wait_send())
 
+    for c in range(CHUNKS):
+        if c > 0:
+            load_piece(c).wait()
+        pl.when(has_slow)(lambda: to_slow(0, c).start())
+    for q in range(last):
+        load(0, q).start()
+    for q in range(planes):
+        for k in (1, 2, 3):
+            load(k, q).start()
+
     def clear(ref, index, n):
         def body(i, _):
             ref[(*index, i)] = jnp.zeros(ref.shape[len(index) + 1 :], ref.dtype)
@@ -150,9 +173,6 @@
             for t in range(STEPS):
                 clear(halo, (t, side), planes)
 
-    load(0, last).wait()
-    for c in range(CHUNKS):
-        pl.when(has_slow)(lambda: to_slow(0, c).start())
     load(0, 0).wait()
     to_fast(0).start()
     for q in range(1, last):
@@ -170,6 +190,8 @@
 
     for q in range(planes):
         pack(0, q)
+    answers = has_lon[1].astype(jnp.int32) + has_lev[1].astype(jnp.int32)
+    pl.when(answers > 0)(lambda: pl.semaphore_wait(above_sem, answers))
     for g in (0, 1):
         start_edges(0, g)
 
@@ -178,85 +200,106 @@
         for t in range(STEPS):
             clear(field, (slot(t, planes),), length + 2)
 
-    level = lax.broadcasted_iota(jnp.int32, (depth, members), 0)
-
-    def cells(t, q, x):
-        here = slot(t, q)
-        cur = field[here, x + 1]
-        below = jnp.where(level == 0, halo[t, 0, q, pl.ds(x, 1), :], pltpu.roll(cur, 1, 0))
-        above = jnp.where(
-            level == depth - 1, halo[t, 1, q, pl.ds(x, 1), :], pltpu.roll(cur, depth - 1, 0)
-        )
+    def cells(t, q, x, z, rows):
+        here, zs = slot(t, q), pl.ds(z, rows)
+        level = lax.broadcasted_iota(jnp.int32, (rows, members), 0)
+        cur = field[here, x + 1, zs]
+        if z == 0:
+            low = halo[t, 0, q, pl.ds(x, 1), :]
+        else:
+            low = field[here, x + 1, pl.ds(z - 1, 1), :]
+        if z + rows == depth:
+            high = halo[t, 1, q, pl.ds(x, 1), :]
+        else:
+            high = field[here, x + 1, pl.ds(z + rows, 1), :]
+        below = jnp.where(level == 0, low, pltpu.roll(cur, 1, 0))
+        above = jnp.where(level == rows - 1, high, pltpu.roll(cur, rows - 1, 0))
         return march(
-            cur, field[slot(t, q + 1), x + 1], field[slot(t, q - 1), x + 1],
-            field[here, x + 2], field[here, x], above, below,
-            winds[0, q, x], winds[1, q, x], winds[2, q, x], sign,
-        )
-
-    def run(t, q, first, n):
+            cur, field[slot(t, q + 1), x + 1, zs], field[slot(t, q - 1), x + 1, zs],
+            field[here, x + 2, zs], field[here, x, zs], above, below,
+            winds[0, q, x, zs], winds[1, q, x, zs], winds[2, q, x, zs], sign,
+        )
+
+    def run(t, q, z, rows):
+        width = UNROLL if rows == depth else UNROLL_PIECE
+
         def body(i, _):
-            for j in range(UNROLL):
-                x = first + i * UNROLL + j
-                new = cells(t, q, x)
-                field[slot(t + 1, q), x + 1] = new
-                face[t + 1, 0, q, pl.ds(x, 1), :] = new[:1]
-                face[t + 1, 1, q, pl.ds(x, 1), :] = new[depth - 1 :]
+            for j in range(width):
+                x = i * width + j
+                new = cells(t, q, x, z, rows)
+                field[slot(t + 1, q), x + 1, pl.ds(z, rows)] = new
+                if z == 0:
+                    face[t + 1, 0, q, pl.ds(x, 1), :] = new[:1]
+                if z + rows == depth:
+                    face[t + 1, 1, q, pl.ds(x, 1), :] = new[rows - 1 :]
             return 0
 
-        lax.fori_loop(0, n // UNROLL, body, 0)
-
-    def run_end(t, q, first, n, sums):
-        guess = field[slot(t, q), length // 2]
+        lax.fori_loop(0, length // width, body, 0)
+
+    def run_end(t, q, z, rows):
+        width = UNROLL if rows == depth else UNROLL_PIECE
+        zs = pl.ds(z, rows)
+        guess = field[slot(t, q), length // 2, zs]
 
         def body(i, sums):
             total, squares = sums
-            for j in range(UNROLL):
-                x = first + i * UNROLL + j
-                new = cells(t, q, x)
-                end[row(q), x] = new
+            for j in range(width):
+                x = i * width + j
+                new = cells(t, q, x, z, rows)
+                end[row(q), x, zs] = new
                 moved = new - guess
                 total = total + moved
                 squares = squares + moved * moved
             return total, squares
 
-        return lax.fori_loop(0, n // UNROLL, body, sums)
-
-    def summarise(t, q, sums):
-        total, squares = sums
-        guess = field[slot(t, q), length // 2]
+        zero = jnp.zeros((rows, members), jnp.float32)
+        total, squares = lax.fori_loop(0, length // width, body, (zero, zero))
         mean = total * (1.0 / length)
-        mine[q, 0] = guess + mean
-        mine[q, 1] = squares - total * mean
-
-    zero = jnp.zeros((depth, members), jnp.float32)
+        mine[q, 0, zs] = guess + mean
+        mine[q, 1, zs] = squares - total * mean
+
+    def combine(q, z, rows):
+        zs = pl.ds(z, rows)
+        means = [mine[q, 0, zs], *(theirs[d, q, 0, zs] for d in range(n_lon - 1))]
+        parts = [mine[q, 1, zs], *(theirs[d, q, 1, zs] for d in range(n_lon - 1))]
+        mean = sum(means) * (1.0 / n_lon)
+        apart = sum((m - mean) * (m - mean) for m in means)
+        variance = (sum(parts) + length * apart) * (1.0 / (length * n_lon))
+        stats[row(q), 0, zs] = mean
+        stats[row(q), 1, zs] = lax.rsqrt(variance + 0.0001)
+
     for t in range(STEPS):
         final = t == STEPS - 1
         if t > 0:
             to_fast(t - 1).wait_send()
         to_fast(t).wait_recv()
-        for g in (0, 1):
-            wait_edges(t, g)
-            if t > 0:
-                wait_edges_sent(t - 1, g)
+        wait_edges(t, 0)
+        if t > 0:
+            wait_edges_sent(t - 1, 0)
         for q in range(last):
             if t == 0:
                 for k in (1, 2, 3):
                     load(k, q).wait()
             if final:
-                summarise(t, q, run_end(t, q, 0, length, (zero, zero)))
+                run_end(t, q, 0, depth)
             else:
-                run(t, q, 0, length)
+                run(t, q, 0, depth)
                 if q == 0:
                     to_fast(t + 1).start()
         if final:
+            to_fast(t).wait_send()
+            for g in (0, 1):
+                wait_edges_sent(t, g)
             for d in range(1, n_lon):
-                to_stat(d, 0).start()
+                to_stat(d, CHUNKS).start()
         else:
             start_edges(t + 1, 0)
+        wait_edges(t, 1)
+        if t > 0:
+            wait_edges_sent(t - 1, 1)
         if t == 0:
             for k in (1, 2, 3):
                 load(k, last).wait()
-        sums = (zero, zero)
         for c in range(CHUNKS):
 
             @pl.when(has_slow)
@@ -266,52 +309,55 @@
                 to_slow(t, c).wait_recv()
 
             if final:
-                sums = run_end(t, last, c * part, part, sums)
+                run_end(t, last, c * part, part)
+                for d in range(1, n_lon):
+                    to_stat(d, c).start()
+                if c == 0:
+                    for d in range(1, n_lon):
+                        to_stat(d, CHUNKS).wait()
+                    for q in range(last):
+                        combine(q, 0, depth)
+                else:
+                    for d in range(1, n_lon):
+                        to_stat(d, c - 1).wait()
+                    combine(last, (c - 1) * part, part)
             else:
                 run(t, last, c * part, part)
                 pl.when(has_slow)(lambda: to_slow(t + 1, c).start())
-        if final:
-            summarise(t, last, sums)
-            for d in range(1, n_lon):
-                to_stat(d, 1).start()
-        else:
+        if not final:
             start_edges(t + 1, 1)
 
-    t = STEPS - 1
     for c in range(CHUNKS):
         pl.when(has_slow)(lambda: to_slow(t, c).wait_send())
-    to_fast(t).wait_send()
-    for g in (0, 1):
-        wait_edges_sent(t, g)
-    for g in (0, 1):
-        for d in range(1, n_lon):
-            to_stat(d, g).wait()
-    for q in range(planes):
-        means = [mine[q, 0], *(theirs[d, q, 0] for d in range(n_lon - 1))]
-        parts = [mine[q, 1], *(theirs[d, q, 1] for d in range(n_lon - 1))]
-        mean = sum(means) * (1.0 / n_lon)
-        apart = sum((m - mean) * (m - mean) for m in means)
-        variance = (sum(parts) + length * apart) * (1.0 / (length * n_lon))
-        stats[row(q), 0] = mean
-        stats[row(q), 1] = lax.rsqrt(variance + 0.0001)
+    for d in range(1, n_lon):
+        to_stat(d, CHUNKS - 1).wait()
+    combine(last, (CHUNKS - 1) * part, part)
 
 
 def normalise(end, stats, normalised, final, scratch, sem):
     planes, length = end.shape[:2]
-    copies = [pltpu.make_async_copy(end, final, sem.at[planes])]
-    copies[0].start()
+    part = length // PARTS
+    copies = [
+        pltpu.make_async_copy(end.at[p], final.at[p], sem.at[0, p, 0]) for p in range(planes)
+    ]
+    for copy in copies:
+        copy.start()
     for p in range(planes):
         mean, scale = stats[p, 0], stats[p, 1]
-
-        def body(i, _, p=p, mean=mean, scale=scale):
-            for j in range(UNROLL):
-                x = i * UNROLL + j
-                scratch[p, x] = (end[p, x] - mean) * scale
-            return 0
-
-        lax.fori_loop(0, length // UNROLL, body, 0)
-        copies.append(pltpu.make_async_copy(scratch.at[p], normalised.at[p], sem.at[p]))
-        copies[-1].start()
+        for c in range(PARTS):
+
+            def body(i, _, p=p, c=c, mean=mean, scale=scale):
+                for j in range(UNROLL):
+                    x = c * part + i * UNROLL + j
+                    scratch[p, x] = (end[p, x] - mean) * scale
+                return 0
+
+            lax.fori_loop(0, part // UNROLL, body, 0)
+            xs = pl.ds(c * part, part)
+            copies.append(
+                pltpu.make_async_copy(scratch.at[p, xs], normalised.at[p, xs], sem.at[1, p, c])
+            )
+            copies[-1].start()
     for copy in copies:
         copy.wait()
 
@@ -340,11 +386,13 @@
             pltpu.VMEM((planes, 2, depth, members), f32),
             pltpu.VMEM((n_lon - 1, planes, 2, depth, members), f32),
             dma((4, planes)),
+            dma((CHUNKS,)),
             dma((STEPS, CHUNKS)), dma((STEPS, CHUNKS)),
             dma((STEPS,)), dma((STEPS,)),
             dma((STEPS, 2, 2)), dma((STEPS, 2, 2)),
             dma((STEPS, 2, 2)), dma((STEPS, 2, 2)),
-            dma((2, n_lon - 1)), dma((2, n_lon - 1)),
+            dma((CHUNKS + 1, n_lon - 1)), dma((CHUNKS + 1, n_lon - 1)),
+            pltpu.SemaphoreType.REGULAR,
         ],
         compiler_params=pltpu.CompilerParams(
             collective_id=0, has_side_effects=True, vmem_limit_bytes=54 * 1024 * 1024
@@ -357,7 +405,7 @@
         out_shape=(jax.ShapeDtypeStruct(block, f32), jax.ShapeDtypeStruct(block, f32)),
         in_specs=[vmem, vmem],
         out_specs=(anywhere, anywhere),
-        scratch_shapes=[pltpu.VMEM(block, f32), dma((planes + 1,))],
+        scratch_shapes=[pltpu.VMEM(block, f32), dma((2, planes, PARTS))],
         compiler_params=pltpu.CompilerParams(vmem_limit_bytes=32 * 1024 * 1024),
         name="normalise",
     )(end, stats)

time: 85 us -> 83.7 us (0.985)
  Pallas kernels: 84.3 us -> 82.9 us
    pallas_call x1, Pallas kernels: 79.6 us -> 78.2 us  [shards(): pl.pallas_call(advance, out_shape=(pltpu.VMEM(block, f32), pltpu.VMEM((pl...]
where the time goes in v2:
time: 83.7 us; the launch traced here: 83.5 us
  Pallas kernels  82.9 us (99%)
    pallas_call x1, Pallas kernels, shards(): pl.pallas_call(advance, out_shape=(pltpu.VMEM(block, f32), pltpu.VMEM((pl...  78.2 us
    pallas_call x1, Pallas kernels, shards(): pl.pallas_call(normalise, out_shape=(jax.ShapeDtypeStruct(block, f32), ja...  4.7 us

profile of v2, /device:TPU:1, one launch (start us, length us, event | category | flops | bytes accessed | tf_op | source)
XLA Modules:
  0.0 83.5 jit_solution(10955753633145218835)
XLA Ops:
  0.6 78.2 %advance.1 = (f32[4,96,32,128]{3,2,1,0:T(8,128)S(1)}, f32[4,2,32,128]{3,2,1,0:T(8,128)S(1)}) custom-call(f32[4,96,32,128]{3,2,1,0:T(8,128)} %state.1, f32[4,96,32,128]{3,2,1,0:T(8,128)} %north.1, f32[4,96,32,128]{3,2,1,0:T(8,128)} %east.1, f32[4,96,32,128]{3,2,1,0:T(8,128)} %upward.1), custom_call_target="tpu_custom_call" | custom-call | tf_op jit(solution)/shard_map/advance/pallas_call | solution.py:373
  78.8 4.7 %normalise.1 = (f32[4,96,32,128]{3,2,1,0:T(8,128)}, f32[4,96,32,128]{3,2,1,0:T(8,128)}) custom-call(f32[4,96,32,128]{3,2,1,0:T(8,128)S(1)} %get-tuple-element.4.end, f32[4,2,32,128]{3,2,1,0:T(8,128)S(1)} %get-tuple-element.5.stats), custom_call_target="tpu_custom_call" | custom-call | tf_op jit(solution)/shard_map/normalise/pallas_call | solution.py:403

commit v3 on v2

--- a/solution.py
+++ b/solution.py
@@ -88,11 +88,17 @@
     pl.when(has_lon[0])(lambda: answer(lon=lon - 1))
     pl.when(has_lev[0])(lambda: answer(lev=lev - 1))
 
-    def to_slow(t, c):
-        xs, zs = pl.ds(1, length), pl.ds(c * part, part)
+    def pieces(t, c):
+        if t == STEPS - 1 and c == CHUNKS - 1:
+            return ((c, 0, length // 2), (CHUNKS, length // 2, length // 2))
+        return ((c, 0, length),)
+
+    def to_slow(t, c, piece):
+        s, x, n = piece
+        xs, zs = pl.ds(1 + x, n), pl.ds(c * part, part)
         return pltpu.make_async_remote_copy(
             field.at[slot(t, last), xs, zs], field.at[slot(t, planes), xs, zs],
-            slow_s.at[t, c], slow_r.at[t, c], device_id={"lat": slow}, device_id_type=MESH,
+            slow_s.at[t, s], slow_r.at[t, s], device_id={"lat": slow}, device_id_type=MESH,
         )
 
     def to_fast(t):
@@ -146,7 +152,7 @@
     for c in range(CHUNKS):
         if c > 0:
             load_piece(c).wait()
-        pl.when(has_slow)(lambda: to_slow(0, c).start())
+        pl.when(has_slow)(lambda: to_slow(0, c, *pieces(0, c)).start())
     for q in range(last):
         load(0, q).start()
     for q in range(planes):
@@ -236,7 +242,7 @@
 
         lax.fori_loop(0, length // width, body, 0)
 
-    def run_end(t, q, z, rows):
+    def run_end(t, q, z, rows, first, n, sums):
         width = UNROLL if rows == depth else UNROLL_PIECE
         zs = pl.ds(z, rows)
         guess = field[slot(t, q), length // 2, zs]
@@ -244,7 +250,7 @@
         def body(i, sums):
             total, squares = sums
             for j in range(width):
-                x = i * width + j
+                x = first + i * width + j
                 new = cells(t, q, x, z, rows)
                 end[row(q), x, zs] = new
                 moved = new - guess
@@ -252,8 +258,11 @@
                 squares = squares + moved * moved
             return total, squares
 
-        zero = jnp.zeros((rows, members), jnp.float32)
-        total, squares = lax.fori_loop(0, length // width, body, (zero, zero))
+        if sums is None:
+            sums = (jnp.zeros((rows, members), jnp.float32),) * 2
+        total, squares = sums = lax.fori_loop(0, n // width, body, sums)
+        if first + n < length:
+            return sums
         mean = total * (1.0 / length)
         mine[q, 0, zs] = guess + mean
         mine[q, 1, zs] = squares - total * mean
@@ -281,7 +290,7 @@
                 for k in (1, 2, 3):
                     load(k, q).wait()
             if final:
-                run_end(t, q, 0, depth)
+                run_end(t, q, 0, depth, 0, length, None)
             else:
                 run(t, q, 0, depth)
                 if q == 0:
@@ -305,12 +314,16 @@
             @pl.when(has_slow)
             def _(c=c):
                 if t > 0:
-                    to_slow(t - 1, c).wait_send()
-                to_slow(t, c).wait_recv()
+                    to_slow(t - 1, c, *pieces(t - 1, c)).wait_send()
+                to_slow(t, c, pieces(t, c)[0]).wait_recv()
 
             if final:
-                run_end(t, last, c * part, part)
-                for d in range(1, n_lon):
+                sums = None
+                for piece in pieces(t, c):
+                    if piece[1] > 0:
+                        pl.when(has_slow)(lambda: to_slow(t, c, piece).wait_recv())
+                    sums = run_end(t, last, c * part, part, *piece[1:], sums)
+                for d in sorted(range(1, n_lon), key=lambda d: -min(d, n_lon - d)):
                     to_stat(d, c).start()
                 if c == 0:
                     for d in range(1, n_lon):
@@ -323,12 +336,17 @@
                     combine(last, (c - 1) * part, part)
             else:
                 run(t, last, c * part, part)
-                pl.when(has_slow)(lambda: to_slow(t + 1, c).start())
+
+                @pl.when(has_slow)
+                def _(c=c):
+                    for piece in pieces(t + 1, c):
+                        to_slow(t + 1, c, piece).start()
         if not final:
             start_edges(t + 1, 1)
 
     for c in range(CHUNKS):
-        pl.when(has_slow)(lambda: to_slow(t, c).wait_send())
+        for piece in pieces(t, c):
+            pl.when(has_slow)(lambda: to_slow(t, c, piece).wait_send())
     for d in range(1, n_lon):
         to_stat(d, CHUNKS - 1).wait()
     combine(last, (CHUNKS - 1) * part, part)
@@ -387,7 +405,7 @@
             pltpu.VMEM((n_lon - 1, planes, 2, depth, members), f32),
             dma((4, planes)),
             dma((CHUNKS,)),
-            dma((STEPS, CHUNKS)), dma((STEPS, CHUNKS)),
+            dma((STEPS, CHUNKS + 1)), dma((STEPS, CHUNKS + 1)),
             dma((STEPS,)), dma((STEPS,)),
             dma((STEPS, 2, 2)), dma((STEPS, 2, 2)),
             dma((STEPS, 2, 2)), dma((STEPS, 2, 2)),

time: 83.7 us -> 83.5 us (level)
  no operation moved by 1% of the time
where the time goes in v3:
time: 83.5 us; the launch traced here: 83.3 us
  Pallas kernels  82.7 us (99%)
    pallas_call x1, Pallas kernels, shards(): pl.pallas_call(advance, out_shape=(pltpu.VMEM(block, f32), pltpu.VMEM((pl...  78 us
    pallas_call x1, Pallas kernels, shards(): pl.pallas_call(normalise, out_shape=(jax.ShapeDtypeStruct(block, f32), ja...  4.7 us

profile of v3, /device:TPU:1, one launch (start us, length us, event | category | flops | bytes accessed | tf_op | source)
XLA Modules:
  0.0 83.3 jit_solution(7991755478650308125)
XLA Ops:
  0.6 78.0 %advance.1 = (f32[4,96,32,128]{3,2,1,0:T(8,128)S(1)}, f32[4,2,32,128]{3,2,1,0:T(8,128)S(1)}) custom-call(f32[4,96,32,128]{3,2,1,0:T(8,128)} %state.1, f32[4,96,32,128]{3,2,1,0:T(8,128)} %north.1, f32[4,96,32,128]{3,2,1,0:T(8,128)} %east.1, f32[4,96,32,128]{3,2,1,0:T(8,128)} %upward.1), custom_call_target="tpu_custom_call" | custom-call | tf_op jit(solution)/shard_map/advance/pallas_call | solution.py:391
  78.6 4.7 %normalise.1 = (f32[4,96,32,128]{3,2,1,0:T(8,128)}, f32[4,96,32,128]{3,2,1,0:T(8,128)}) custom-call(f32[4,96,32,128]{3,2,1,0:T(8,128)S(1)} %get-tuple-element.4.end, f32[4,2,32,128]{3,2,1,0:T(8,128)S(1)} %get-tuple-element.5.stats), custom_call_target="tpu_custom_call" | custom-call | tf_op jit(solution)/shard_map/normalise/pallas_call | solution.py:421
